TPU v7x, 32 devices: a whole 2x2x4 slice. The times are simulated.
32 devices in a mesh: ep: 8 (over z, y), dp: 4 (over x, core).
Axes of the slice: x: 2, y: 2, z: 4, core: 2. Of those that a mesh axis runs over, the one named last changes fastest.
Arguments:
- tokens: bfloat16 [512, 7168], P(('ep', 'dp')), may hold values from -6 to 6
- routes: int32 [512, 2], P(('ep', 'dp')), may hold values from 0 to 7, all different within a row; in each aligned block of 16 rows (0 to 15, 16 to 31, ...) at most 8 rows name the same one
- route_logits: float32 [512, 2], P(('ep', 'dp')), may hold values from -6 to 6
- gate_weight: bfloat16 [8, 7168, 2048], P('ep', None, 'dp'), may hold values from -0.0625 to 0.0625
- up_weight: bfloat16 [8, 7168, 2048], P('ep', None, 'dp'), may hold values from -0.0625 to 0.0625
- down_weight: bfloat16 [8, 2048, 7168], P('ep', 'dp'), may hold values from -0.125 to 0.125
Outputs:
- moe_output: bfloat16 [512, 7168], P(('ep', 'dp'))
- expert_load: float32 [8], P('ep')
Inputs may be any that keep to these rules, and one draw needn't show every extreme that they name: `routes`: each row names 2 different experts. Within the rows of one device (aligned blocks of 16 rows) no expert is named more than 8 times, and in every draw some expert is named exactly 8 times there; every expert is named somewhere.
All inputs are finite; a program needn't handle non-finite values.
Results may differ from a plain program's by a relative error of at most 0.012.
Values may be sent and summed in bfloat16 or wider, within the bound.
A program may use at most 128 MiB of HBM per device.

v0:
```python
import functools

import jax
import jax.numpy as jnp
from jax import lax
from jax.experimental import pallas as pl
from jax.experimental.pallas import tpu as pltpu
from jax.sharding import PartitionSpec as P

ROUTE_SCALE = 2.5
PRECISE = lax.Precision.HIGHEST


def assignment_slots(flat_routes, experts):
    labels = jnp.arange(experts, dtype=jnp.int32)
    onehot = (flat_routes[:, :, None] == labels[None, None, :]).astype(jnp.int32)
    before = jnp.cumsum(onehot, axis=1) - onehot
    return (jnp.sum(before * onehot, axis=2), jnp.sum(onehot, axis=1))


def pack(members, flat_routes, slot_ids, experts, capacity, top_k):
    blocks, per_block = flat_routes.shape
    tok_dev = per_block // top_k
    member = jnp.arange(blocks, dtype=jnp.int32)[:, None]
    target = ((member * experts + flat_routes) * capacity + slot_ids).reshape(-1)
    source = (member * tok_dev + jnp.arange(per_block, dtype=jnp.int32)[None, :] // top_k).reshape(
        -1
    )
    placing = (
        jnp.arange(blocks * experts * capacity, dtype=jnp.int32)[:, None] == target[None, :]
    ).astype(jnp.bfloat16)
    owners = (source[:, None] == jnp.arange(blocks * tok_dev, dtype=jnp.int32)[None, :]).astype(
        jnp.bfloat16
    )
    picker = jnp.dot(placing, owners, preferred_element_type=jnp.float32).astype(jnp.bfloat16)
    filled = jnp.dot(picker, members, preferred_element_type=jnp.float32).astype(jnp.bfloat16)
    return filled.reshape(blocks, experts, capacity, members.shape[1])


def expert_rows(row_block, gate_w, up_w, down_w):
    gate_act = jnp.dot(row_block, gate_w, preferred_element_type=jnp.float32)
    up_act = jnp.dot(row_block, up_w, preferred_element_type=jnp.float32)
    hidden = (jax.nn.silu(gate_act) * up_act).astype(jnp.bfloat16)
    return jnp.dot(hidden, down_w, preferred_element_type=jnp.float32)


def on_device(tokens, routes, route_logits, gate_weight, up_weight, down_weight):
    tok_dev, top_k = routes.shape
    model_width = tokens.shape[1]
    experts = lax.axis_size("ep")
    groups = lax.axis_size("dp")
    capacity = min(tok_dev // 2, 2 * tok_dev * top_k // experts)
    per_block = tok_dev * top_k
    gate_w = gate_weight[0]
    up_w = up_weight[0]
    down_w = down_weight[0]
    own_flat = routes.reshape(1, per_block)
    own_slots, own_counts = assignment_slots(own_flat, experts)
    buffer = pack(tokens, own_flat, own_slots, experts, capacity, top_k)
    received = lax.all_to_all(buffer, "ep", split_axis=1, concat_axis=1, tiled=True)
    partial_value = expert_rows(
        lax.all_gather(received.reshape(-1, model_width), "dp", axis=0, tiled=True),
        gate_w,
        up_w,
        down_w,
    )
    shares = lax.psum_scatter(
        partial_value.astype(jnp.bfloat16), "dp", scatter_dimension=0, tiled=True
    ).astype(jnp.float32)
    returned = lax.all_to_all(
        shares.reshape(experts, capacity, model_width).astype(jnp.bfloat16),
        "ep",
        split_axis=0,
        concat_axis=0,
        tiled=True,
    ).astype(jnp.float32)
    affinity = jax.nn.sigmoid(route_logits)
    weights = (ROUTE_SCALE * affinity / jnp.sum(affinity, axis=1, keepdims=True)).reshape(-1)
    own_target = own_flat[0] * capacity + own_slots[0]
    spread = jnp.where(
        own_target[:, None] == jnp.arange(experts * capacity, dtype=jnp.int32)[None, :],
        weights[:, None],
        0.0,
    )
    owners = (
        jnp.arange(tok_dev, dtype=jnp.int32)[:, None]
        == jnp.arange(per_block, dtype=jnp.int32)[None, :] // top_k
    ).astype(jnp.float32)
    combine = jnp.dot(owners, spread, precision=PRECISE)
    moe_output = jnp.dot(
        combine, returned.reshape(experts * capacity, model_width), precision=PRECISE
    ).astype(jnp.bfloat16)
    local_counts = own_counts[0].astype(jnp.float32)
    whole = lax.psum(local_counts, ("ep", "dp"))
    expert_count = lax.dynamic_slice_in_dim(whole, lax.axis_index("ep"), 1)
    mean_count = float(tok_dev * groups * top_k)
    expert_load = expert_count / mean_count
    return (moe_output, expert_load)


MESH = pl.DeviceIdType.MESH
WINDOW = 2
X_LAG = 2
B_LAG = 4
R_LAG = 2


def chunk_count(width):
    for count in (7, 8, 4, 2):
        if width % (count * 128) == 0:
            return count
    return 1


def remote(src, dst, send, recv, ep, dp):
    return pltpu.make_async_remote_copy(
        src_ref=src,
        dst_ref=dst,
        send_sem=send,
        recv_sem=recv,
        device_id={"ep": ep, "dp": dp},
        device_id_type=MESH,
    )


def fused_kernel(
    E, G, cap, nc, dc, mean_count,
    routes_t, logits_t, tokens, wg_hbm, wu_hbm, wd_hbm,
    out, load,
    wg, wu, wd, slots, rows, acc_g, acc_u, hidden, part, a_recv, b_send, b_recv, r_send, r_recv,
    combine, cnt_send, cnt_recv, dcnt_send, dcnt_recv,
    w_sem, s1_send, s1_recv, x_send, x_recv, c_send, c_recv,
    ra_send, ra_recv, rb_send, rb_recv, rr_send, rr_recv,
    n_send, n_recv, nd_send, nd_recv,
):
    me = lax.axis_index("ep")
    dp = lax.axis_index("dp")
    hi = dp // 2
    lo = dp % 2
    px = (1 - hi) * 2 + lo
    pc = hi * 2 + (1 - lo)
    top, tok = routes_t.shape
    n_slots = E * cap

    def peers(body):
        def step(k, carry):
            body(lax.rem(me + k, E))
            return carry

        lax.fori_loop(1, E, step, 0)

    barrier = pltpu.get_barrier_semaphore()
    peers(lambda e: pl.semaphore_signal(
        barrier, inc=1, device_id={"ep": e, "dp": dp}, device_id_type=MESH))
    pl.semaphore_signal(barrier, inc=1, device_id={"ep": me, "dp": px}, device_id_type=MESH)
    pl.semaphore_signal(barrier, inc=1, device_id={"ep": me, "dp": pc}, device_id_type=MESH)

    def weight_copies(c):
        cols = pl.ds(pl.multiple_of(c * dc, 128), dc)
        return (
            pltpu.make_async_copy(wg_hbm.at[0, cols], wg.at[c], w_sem.at[0, c]),
            pltpu.make_async_copy(wu_hbm.at[0, cols], wu.at[c], w_sem.at[1, c]),
            pltpu.make_async_copy(wd_hbm.at[0, :, cols], wd.at[c], w_sem.at[2, c]),
        )

    def start_weights(c, carry):
        copies = weight_copies(c)
        copies[0].start()
        copies[1].start()
        return carry

    def start_down(c, carry):
        weight_copies(c)[2].start()
        return carry

    lax.fori_loop(0, nc, start_weights, 0)
    lax.fori_loop(0, nc, start_down, 0)

    slot_row = lax.broadcasted_iota(jnp.int32, (n_slots, tok), 0)
    named = jnp.zeros((n_slots, tok), jnp.float32)
    for k in range(top):
        named = named + jnp.where(routes_t[k:k + 1, :] == slot_row // cap, 1.0, 0.0)
    earlier = jnp.where(
        lax.broadcasted_iota(jnp.int32, (tok, tok), 0)
        < lax.broadcasted_iota(jnp.int32, (tok, tok), 1), 1.0, 0.0)
    before = jnp.dot(named, earlier, preferred_element_type=jnp.float32)
    placed = before == (slot_row % cap).astype(jnp.float32)
    picker = jnp.where(placed, named, 0.0).astype(jnp.bfloat16)
    counted = jnp.sum(named, axis=1, keepdims=True)
    cnt_send[...] = jnp.broadcast_to(counted, (n_slots, 128)).reshape(E, cap, 128)

    def pack_chunk(c, carry):
        cols = pl.ds(pl.multiple_of(c * dc, 128), dc)
        filled = jnp.dot(picker, tokens[:, cols], preferred_element_type=jnp.float32)
        slots[c] = filled.reshape(E, cap, dc).astype(jnp.bfloat16)
        rows[c, dp, me] = slots[c, me]
        return carry

    lax.fori_loop(0, nc, pack_chunk, 0)
    cnt_recv[me] = cnt_send[me]

    def first(c, src, dst_e):
        return remote(slots.at[c, dst_e], rows.at[c, dp, src],
                      s1_send.at[c, dst_e], s1_recv.at[c, src], dst_e, dp)

    def counts(src, dst_e):
        return remote(cnt_send.at[dst_e], cnt_recv.at[src],
                      n_send.at[dst_e], n_recv.at[src], dst_e, dp)

    pl.semaphore_wait(barrier, E + 1)

    def send_first(c, carry):
        peers(lambda e: first(c, me, e).start())
        return carry

    lax.fori_loop(0, min(WINDOW, nc), send_first, 0)
    peers(lambda e: counts(me, e).start())

    affinity = jax.nn.sigmoid(logits_t[...])
    weights = ROUTE_SCALE * affinity / jnp.sum(affinity, axis=0, keepdims=True)
    spread = jnp.zeros((n_slots, tok), jnp.float32)
    for k in range(top):
        hit = routes_t[k:k + 1, :] == slot_row // cap
        spread = spread + jnp.where(hit, weights[k:k + 1, :], 0.0)
    spread = jnp.where(placed, spread, 0.0)
    coarse = spread.astype(jnp.bfloat16)
    rest = spread - coarse.astype(jnp.float32)
    middle = rest.astype(jnp.bfloat16)
    fine = (rest - middle.astype(jnp.float32)).astype(jnp.bfloat16)
    same = jnp.where(
        lax.broadcasted_iota(jnp.int32, (tok, tok), 0)
        == lax.broadcasted_iota(jnp.int32, (tok, tok), 1), 1.0, 0.0).astype(jnp.bfloat16)
    for i, piece in enumerate((coarse, middle, fine)):
        turned = lax.dot_general(
            same, piece, (((1,), (1,)), ((), ())), preferred_element_type=jnp.float32)
        combine[i * tok:(i + 1) * tok] = turned.astype(jnp.bfloat16)

    acc_g[...] = jnp.zeros_like(acc_g)
    acc_u[...] = jnp.zeros_like(acc_u)

    def across(c, who):
        return remote(rows.at[c, who], rows.at[c, who], x_send.at[c], x_recv.at[c], me, px)

    def beside(c, i, who):
        return remote(rows.at[c, who], rows.at[c, who],
                      c_send.at[c, i], c_recv.at[c, i], me, pc)

    def forward(s, carry):
        @pl.when(s < nc)
        def _():
            peers(lambda e: first(s, e, me).wait_recv())
            across(s, dp).start()
            beside(s, 0, dp).start()

        @pl.when(s + WINDOW < nc)
        def _():
            send_first(s + WINDOW, 0)

        @pl.when((s >= X_LAG) & (s < nc + X_LAG))
        def _():
            c = s - X_LAG
            across(c, px).wait_recv()
            beside(c, 1, px).start()

        @pl.when(s >= X_LAG + 1)
        def _():
            c = s - X_LAG - 1
            beside(c, 0, pc).wait_recv()
            beside(c, 1, (1 - hi) * 2 + (1 - lo)).wait_recv()
            copies = weight_copies(c)
            copies[0].wait()
            copies[1].wait()
            x = rows[c].astype(jnp.float32).reshape(G * n_slots, dc).astype(jnp.bfloat16)
            acc_g[...] += jnp.dot(x, wg[c], preferred_element_type=jnp.float32)
            acc_u[...] += jnp.dot(x, wu[c], preferred_element_type=jnp.float32)

        return carry

    lax.fori_loop(0, nc + X_LAG + 1, forward, 0)
    gate = acc_g[...]
    hidden[...] = (gate / (1.0 + jnp.exp(-gate)) * acc_u[...]).astype(jnp.bfloat16)

    def half(c, h):
        return remote(part.at[c, h * 2 + (1 - lo)], a_recv.at[c, h],
                      ra_send.at[c, h], ra_recv.at[c, h], me, pc)

    def quarter(c):
        return remote(b_send.at[c], b_recv.at[c], rb_send.at[c], rb_recv.at[c], me, px)

    def back(c, src, dst_e):
        return remote(r_send.at[c, dst_e], r_recv.at[c, src],
                      rr_send.at[c, dst_e], rr_recv.at[c, src], dst_e, dp)

    def wide(value):
        return value.astype(jnp.float32)

    def backward(s, carry):
        @pl.when(s < nc)
        def _():
            weight_copies(s)[2].wait()
            p = jnp.dot(hidden[...], wd[s], preferred_element_type=jnp.float32)
            part[s] = p.reshape(G, E, cap, dc).astype(jnp.bfloat16)
            half(s, 1 - hi).start()
            half(s, hi).start()

        @pl.when((s >= 1) & (s < nc + 1))
        def _():
            c = s - 1
            half(c, 1 - hi).wait_recv()
            total = wide(part[c, px]) + wide(a_recv[c, 1 - hi])
            b_send[c] = total.astype(jnp.bfloat16)
            quarter(c).start()

        @pl.when((s >= B_LAG) & (s < nc + B_LAG))
        def _():
            c = s - B_LAG
            half(c, hi).wait_recv()
            quarter(c).wait_recv()
            total = wide(part[c, dp]) + wide(a_recv[c, hi]) + wide(b_recv[c])
            r_send[c] = total.astype(jnp.bfloat16)
            peers(lambda e: back(c, me, e).start())
            r_recv[c, me] = r_send[c, me]

        @pl.when(s >= B_LAG + R_LAG)
        def _():
            c = s - B_LAG - R_LAG
            peers(lambda e: back(c, e, me).wait_recv())
            got = r_recv[c].astype(jnp.float32).reshape(n_slots, dc).astype(jnp.bfloat16)
            mixed = jnp.dot(combine[...], got, preferred_element_type=jnp.float32)
            total = mixed[0:tok] + mixed[tok:2 * tok] + mixed[2 * tok:3 * tok]
            out[:, pl.ds(pl.multiple_of(c * dc, 128), dc)] = total.astype(jnp.bfloat16)

        return carry

    lax.fori_loop(0, nc + B_LAG + R_LAG, backward, 0)

    peers(lambda e: counts(e, me).wait_recv())
    mine = cnt_recv[0]
    for e in range(1, E):
        mine = mine + cnt_recv[e]
    for i, partner in enumerate((px, pc)):
        dcnt_send[i] = mine
        swap = remote(dcnt_send.at[i], dcnt_recv.at[i], nd_send.at[i], nd_recv.at[i], me, partner)
        swap.start()
        swap.wait_recv()
        mine = mine + dcnt_recv[i]
        swap.wait_send()
    load[...] = mine[0:1, :] / mean_count

    peers(lambda e: counts(me, e).wait_send())

    def drain(c, carry):
        peers(lambda e: first(c, me, e).wait_send())
        across(c, dp).wait_send()
        beside(c, 0, dp).wait_send()
        beside(c, 1, px).wait_send()
        half(c, 1 - hi).wait_send()
        half(c, hi).wait_send()
        quarter(c).wait_send()
        peers(lambda e: back(c, me, e).wait_send())
        return carry

    lax.fori_loop(0, nc, drain, 0)


def fused_device(tokens, routes, route_logits, gate_weight, up_weight, down_weight):
    tok_dev, top_k = routes.shape
    width = tokens.shape[1]
    units = gate_weight.shape[2]
    E = lax.axis_size("ep")
    G = lax.axis_size("dp")
    cap = min(tok_dev // 2, 2 * tok_dev * top_k // E)
    nc = chunk_count(width)
    dc = width // nc
    bf, f32 = jnp.bfloat16, jnp.float32
    dma = pltpu.SemaphoreType.DMA
    vmem = pl.BlockSpec(memory_space=pltpu.VMEM)
    anywhere = pl.BlockSpec(memory_space=pl.ANY)
    rows = G * E * cap
    moe_output, load = pl.pallas_call(
        functools.partial(fused_kernel, E, G, cap, nc, dc, float(tok_dev * G * top_k)),
        out_shape=(
            jax.ShapeDtypeStruct((tok_dev, width), bf),
            jax.ShapeDtypeStruct((1, 128), f32),
        ),
        in_specs=[vmem, vmem, vmem, anywhere, anywhere, anywhere],
        out_specs=(vmem, vmem),
        scratch_shapes=[
            pltpu.VMEM((nc, dc, units), bf),
            pltpu.VMEM((nc, dc, units), bf),
            pltpu.VMEM((nc, units, dc), bf),
            pltpu.VMEM((nc, E, cap, dc), bf),
            pltpu.VMEM((nc, G, E, cap, dc), bf),
            pltpu.VMEM((rows, units), f32),
            pltpu.VMEM((rows, units), f32),
            pltpu.VMEM((rows, units), bf),
            pltpu.VMEM((nc, G, E, cap, dc), bf),
            pltpu.VMEM((nc, 2, E, cap, dc), bf),
            pltpu.VMEM((nc, E, cap, dc), bf),
            pltpu.VMEM((nc, E, cap, dc), bf),
            pltpu.VMEM((nc, E, cap, dc), bf),
            pltpu.VMEM((nc, E, cap, dc), bf),
            pltpu.VMEM((3 * tok_dev, E * cap), bf),
            pltpu.VMEM((E, cap, 128), f32),
            pltpu.VMEM((E, cap, 128), f32),
            pltpu.VMEM((2, cap, 128), f32),
            pltpu.VMEM((2, cap, 128), f32),
            dma((3, nc)),
            dma((nc, E)), dma((nc, E)),
            dma((nc,)), dma((nc,)),
            dma((nc, 2)), dma((nc, 2)),
            dma((nc, 2)), dma((nc, 2)),
            dma((nc,)), dma((nc,)),
            dma((nc, E)), dma((nc, E)),
            dma((E,)), dma((E,)),
            dma((2,)), dma((2,)),
        ],
        compiler_params=pltpu.CompilerParams(
            collective_id=0, has_side_effects=True, vmem_limit_bytes=60 * 2**20
        ),
    )(routes.T, route_logits.T, tokens, gate_weight, up_weight, down_weight)
    return moe_output, load[0, :1]


def fits(mesh):
    return mesh.shape["dp"] == 4 and mesh.shape["ep"] <= 8


def solution(mesh):
    body = fused_device if fits(mesh) else on_device
    return jax.shard_map(
        body,
        mesh=mesh,
        in_specs=(
            P(("ep", "dp"), None),
            P(("ep", "dp"), None),
            P(("ep", "dp"), None),
            P("ep", None, "dp"),
            P("ep", None, "dp"),
            P("ep", "dp", None),
        ),
        out_specs=(P(("ep", "dp"), None), P("ep")),
        check_vma=False,
    )
```

profile of v0, /device:TPU:0, one launch (start us, length us, event | category | flops | bytes accessed | tf_op | source)
XLA Modules:
  0.0 77.4 jit_solution(2729028283607987416)
XLA Ops:
  0.6 73.3 %shard_map.77 = (bf16[16,7168]{1,0:T(8,128)(2,1)}, f32[1,128]{1,0:T(1,128)}) custom-call(s32[2,16]{1,0:T(2,128)} %bitcast.4, f32[2,16]{1,0:T(2,128)} %bitcast.5, bf16[16,7168]{1,0:T(8,128)(2,1)} %tokens.1, bf16[1,7168,512]{2,1,0:T(8,128)(2,1)} %wg_hbm.1, bf16[1,7168,512]{2,1,0:T(8,128)(2,1)} %wu_hbm.1, bf16[1,512,7168]{2,1,0:T(8,128)(2,1)} %wd_hbm.1), custom_call_target="tpu_custom_call" | custom-call | tf_op jit(solution)/shard_map/pallas_call | solution.py:380
  74.0 1.6 %copy.10 = bf16[16,7168]{1,0:T(8,128)(2,1)} copy(bf16[16,7168]{1,0:T(8,128)(2,1)} %get-tuple-element.8) | data formatting | bytes 458752
where the time goes:
time: 77.5 us; the launch traced here: 77.4 us
  Pallas kernels  73.3 us (95%)
  between operations  2.4 us (3%)
  local copies, waits for them, and re-layouts  1.64 us (2%)
    pallas_call x1, Pallas kernels, fused_device(): pl.pallas_call(functools.partial(fused_kernel, E, G, cap, nc, dc, float(t...  73.3 us
    unnamed x1, local copies, waits for them, and re-layouts  1.64 us

commit v1 on v0

--- a/solution.py
+++ b/solution.py
@@ -99,14 +99,16 @@
 
 
 MESH = pl.DeviceIdType.MESH
-WINDOW = 2
-X_LAG = 2
-B_LAG = 4
-R_LAG = 2
+WINDOW = 6
+X_LAG = 3
+C_LAG = 2
+H_LAG = 2
+B_LAG = 6
+R_LAG = 3
 
 
 def chunk_count(width):
-    for count in (7, 8, 4, 2):
+    for count in (14, 7, 8, 4, 2):
         if width % (count * 128) == 0:
             return count
     return 1
@@ -125,11 +127,11 @@
 
 def fused_kernel(
     E, G, cap, nc, dc, mean_count,
-    routes_t, logits_t, tokens, wg_hbm, wu_hbm, wd_hbm,
-    out, load,
+    routes_hbm, logits_hbm, tokens_hbm, wg_hbm, wu_hbm, wd_hbm,
+    out, load, routes_t, logits_t, tokens,
     wg, wu, wd, slots, rows, acc_g, acc_u, hidden, part, a_recv, b_send, b_recv, r_send, r_recv,
     combine, cnt_send, cnt_recv, dcnt_send, dcnt_recv,
-    w_sem, s1_send, s1_recv, x_send, x_recv, c_send, c_recv,
+    in_sem, w_sem, s1_send, s1_recv, x_send, x_recv, c_send, c_recv,
     ra_send, ra_recv, rb_send, rb_recv, rr_send, rr_recv,
     n_send, n_recv, nd_send, nd_recv,
 ):
@@ -139,8 +141,11 @@
     lo = dp % 2
     px = (1 - hi) * 2 + lo
     pc = hi * 2 + (1 - lo)
-    top, tok = routes_t.shape
+    top, tok = routes_hbm.shape
     n_slots = E * cap
+
+    def landed(ref, sem):
+        pltpu.make_async_copy(ref, ref, sem).wait()
 
     def peers(body):
         def step(k, carry):
@@ -154,6 +159,14 @@
         barrier, inc=1, device_id={"ep": e, "dp": dp}, device_id_type=MESH))
     pl.semaphore_signal(barrier, inc=1, device_id={"ep": me, "dp": px}, device_id_type=MESH)
     pl.semaphore_signal(barrier, inc=1, device_id={"ep": me, "dp": pc}, device_id_type=MESH)
+
+    inputs = [
+        pltpu.make_async_copy(src, dst, in_sem.at[i])
+        for i, (src, dst) in enumerate(
+            ((routes_hbm, routes_t), (logits_hbm, logits_t), (tokens_hbm, tokens)))
+    ]
+    for copy in inputs:
+        copy.start()
 
     def weight_copies(c):
         cols = pl.ds(pl.multiple_of(c * dc, 128), dc)
@@ -176,6 +189,8 @@
     lax.fori_loop(0, nc, start_weights, 0)
     lax.fori_loop(0, nc, start_down, 0)
 
+    for copy in inputs:
+        copy.wait()
     slot_row = lax.broadcasted_iota(jnp.int32, (n_slots, tok), 0)
     named = jnp.zeros((n_slots, tok), jnp.float32)
     for k in range(top):
@@ -201,11 +216,11 @@
 
     def first(c, src, dst_e):
         return remote(slots.at[c, dst_e], rows.at[c, dp, src],
-                      s1_send.at[c, dst_e], s1_recv.at[c, src], dst_e, dp)
+                      s1_send, s1_recv.at[c], dst_e, dp)
 
     def counts(src, dst_e):
         return remote(cnt_send.at[dst_e], cnt_recv.at[src],
-                      n_send.at[dst_e], n_recv.at[src], dst_e, dp)
+                      n_send, n_recv, dst_e, dp)
 
     pl.semaphore_wait(barrier, E + 1)
 
@@ -239,16 +254,16 @@
     acc_u[...] = jnp.zeros_like(acc_u)
 
     def across(c, who):
-        return remote(rows.at[c, who], rows.at[c, who], x_send.at[c], x_recv.at[c], me, px)
+        return remote(rows.at[c, who], rows.at[c, who], x_send, x_recv.at[c], me, px)
 
     def beside(c, i, who):
         return remote(rows.at[c, who], rows.at[c, who],
-                      c_send.at[c, i], c_recv.at[c, i], me, pc)
+                      c_send, c_recv.at[c], me, pc)
 
     def forward(s, carry):
         @pl.when(s < nc)
         def _():
-            peers(lambda e: first(s, e, me).wait_recv())
+            landed(rows.at[s, dp, 0:E - 1], s1_recv.at[s])
             across(s, dp).start()
             beside(s, 0, dp).start()
 
@@ -262,11 +277,10 @@
             across(c, px).wait_recv()
             beside(c, 1, px).start()
 
-        @pl.when(s >= X_LAG + 1)
-        def _():
-            c = s - X_LAG - 1
-            beside(c, 0, pc).wait_recv()
-            beside(c, 1, (1 - hi) * 2 + (1 - lo)).wait_recv()
+        @pl.when(s >= X_LAG + C_LAG)
+        def _():
+            c = s - X_LAG - C_LAG
+            landed(rows.at[c, 0:2], c_recv.at[c])
             copies = weight_copies(c)
             copies[0].wait()
             copies[1].wait()
@@ -276,20 +290,27 @@
 
         return carry
 
-    lax.fori_loop(0, nc + X_LAG + 1, forward, 0)
+    lax.fori_loop(0, nc + X_LAG + C_LAG, forward, 0)
+    landed(cnt_recv.at[0:E - 1], n_recv)
+    mine = cnt_recv[0]
+    for e in range(1, E):
+        mine = mine + cnt_recv[e]
+    dcnt_send[...] = mine
+    for i in range(1, G):
+        remote(dcnt_send, dcnt_recv.at[i - 1], nd_send, nd_recv, me, lax.rem(dp + i, G)).start()
     gate = acc_g[...]
     hidden[...] = (gate / (1.0 + jnp.exp(-gate)) * acc_u[...]).astype(jnp.bfloat16)
 
     def half(c, h):
         return remote(part.at[c, h * 2 + (1 - lo)], a_recv.at[c, h],
-                      ra_send.at[c, h], ra_recv.at[c, h], me, pc)
+                      ra_send, ra_recv.at[c, h], me, pc)
 
     def quarter(c):
-        return remote(b_send.at[c], b_recv.at[c], rb_send.at[c], rb_recv.at[c], me, px)
+        return remote(b_send.at[c], b_recv.at[c], rb_send, rb_recv.at[c], me, px)
 
     def back(c, src, dst_e):
         return remote(r_send.at[c, dst_e], r_recv.at[c, src],
-                      rr_send.at[c, dst_e], rr_recv.at[c, src], dst_e, dp)
+                      rr_send, rr_recv.at[c], dst_e, dp)
 
     def wide(value):
         return value.astype(jnp.float32)
@@ -303,9 +324,9 @@
             half(s, 1 - hi).start()
             half(s, hi).start()
 
-        @pl.when((s >= 1) & (s < nc + 1))
-        def _():
-            c = s - 1
+        @pl.when((s >= H_LAG) & (s < nc + H_LAG))
+        def _():
+            c = s - H_LAG
             half(c, 1 - hi).wait_recv()
             total = wide(part[c, px]) + wide(a_recv[c, 1 - hi])
             b_send[c] = total.astype(jnp.bfloat16)
@@ -324,7 +345,7 @@
         @pl.when(s >= B_LAG + R_LAG)
         def _():
             c = s - B_LAG - R_LAG
-            peers(lambda e: back(c, e, me).wait_recv())
+            landed(r_recv.at[c, 0:E - 1], rr_recv.at[c])
             got = r_recv[c].astype(jnp.float32).reshape(n_slots, dc).astype(jnp.bfloat16)
             mixed = jnp.dot(combine[...], got, preferred_element_type=jnp.float32)
             total = mixed[0:tok] + mixed[tok:2 * tok] + mixed[2 * tok:3 * tok]
@@ -334,33 +355,20 @@
 
     lax.fori_loop(0, nc + B_LAG + R_LAG, backward, 0)
 
-    peers(lambda e: counts(e, me).wait_recv())
-    mine = cnt_recv[0]
-    for e in range(1, E):
-        mine = mine + cnt_recv[e]
-    for i, partner in enumerate((px, pc)):
-        dcnt_send[i] = mine
-        swap = remote(dcnt_send.at[i], dcnt_recv.at[i], nd_send.at[i], nd_recv.at[i], me, partner)
-        swap.start()
-        swap.wait_recv()
+    landed(dcnt_recv.at[0:G - 1], nd_recv)
+    mine = dcnt_send[...]
+    for i in range(G - 1):
         mine = mine + dcnt_recv[i]
-        swap.wait_send()
     load[...] = mine[0:1, :] / mean_count
 
-    peers(lambda e: counts(me, e).wait_send())
-
-    def drain(c, carry):
-        peers(lambda e: first(c, me, e).wait_send())
-        across(c, dp).wait_send()
-        beside(c, 0, dp).wait_send()
-        beside(c, 1, px).wait_send()
-        half(c, 1 - hi).wait_send()
-        half(c, hi).wait_send()
-        quarter(c).wait_send()
-        peers(lambda e: back(c, me, e).wait_send())
-        return carry
-
-    lax.fori_loop(0, nc, drain, 0)
+    landed(cnt_recv.at[0:E - 1], n_send)
+    landed(dcnt_recv.at[0:G - 1], nd_send)
+    landed(slots.at[:, 0:E - 1], s1_send)
+    landed(b_send, x_send)
+    landed(a_recv, c_send)
+    landed(a_recv, ra_send)
+    landed(b_send, rb_send)
+    landed(r_send.at[:, 0:E - 1], rr_send)
 
 
 def fused_device(tokens, routes, route_logits, gate_weight, up_weight, down_weight):
@@ -383,9 +391,12 @@
             jax.ShapeDtypeStruct((tok_dev, width), bf),
             jax.ShapeDtypeStruct((1, 128), f32),
         ),
-        in_specs=[vmem, vmem, vmem, anywhere, anywhere, anywhere],
+        in_specs=[anywhere] * 6,
         out_specs=(vmem, vmem),
         scratch_shapes=[
+            pltpu.VMEM((top_k, tok_dev), jnp.int32),
+            pltpu.VMEM((top_k, tok_dev), f32),
+            pltpu.VMEM((tok_dev, width), bf),
             pltpu.VMEM((nc, dc, units), bf),
             pltpu.VMEM((nc, dc, units), bf),
             pltpu.VMEM((nc, units, dc), bf),
@@ -403,17 +414,18 @@
             pltpu.VMEM((3 * tok_dev, E * cap), bf),
             pltpu.VMEM((E, cap, 128), f32),
             pltpu.VMEM((E, cap, 128), f32),
-            pltpu.VMEM((2, cap, 128), f32),
-            pltpu.VMEM((2, cap, 128), f32),
+            pltpu.VMEM((cap, 128), f32),
+            pltpu.VMEM((G - 1, cap, 128), f32),
+            dma((3,)),
             dma((3, nc)),
-            dma((nc, E)), dma((nc, E)),
-            dma((nc,)), dma((nc,)),
-            dma((nc, 2)), dma((nc, 2)),
-            dma((nc, 2)), dma((nc, 2)),
-            dma((nc,)), dma((nc,)),
-            dma((nc, E)), dma((nc, E)),
-            dma((E,)), dma((E,)),
-            dma((2,)), dma((2,)),
+            dma, dma((nc,)),
+            dma, dma((nc,)),
+            dma, dma((nc,)),
+            dma, dma((nc, 2)),
+            dma, dma((nc,)),
+            dma, dma((nc,)),
+            dma, dma,
+            dma, dma,
         ],
         compiler_params=pltpu.CompilerParams(
             collective_id=0, has_side_effects=True, vmem_limit_bytes=60 * 2**20

time: 77.5 us -> 70.2 us (0.906)
  Pallas kernels: 73.3 us -> 66 us
    pallas_call x1, Pallas kernels: 73.3 us -> 66 us  [fused_device(): pl.pallas_call(functools.partial(fused_kernel, E, G, cap, nc, dc, float(t...]
where the time goes in v1:
time: 70.2 us; the launch traced here: 70 us
  Pallas kernels  66 us (94%)
  between operations  2.4 us (3%)
  local copies, waits for them, and re-layouts  1.64 us (2%)
    pallas_call x1, Pallas kernels, fused_device(): pl.pallas_call(functools.partial(fused_kernel, E, G, cap, nc, dc, float(t...  66 us
    unnamed x1, local copies, waits for them, and re-layouts  1.64 us

profile of v1, /device:TPU:0, one launch (start us, length us, event | category | flops | bytes accessed | tf_op | source)
XLA Modules:
  0.0 70.0 jit_solution(3715535144781130577)
XLA Ops:
  0.6 66.0 %shard_map.77 = (bf16[16,7168]{1,0:T(8,128)(2,1)}, f32[1,128]{1,0:T(1,128)}) custom-call(s32[2,16]{1,0:T(2,128)} %bitcast.4, f32[2,16]{1,0:T(2,128)} %bitcast.5, bf16[16,7168]{1,0:T(8,128)(2,1)} %tokens_hbm.1, bf16[1,7168,512]{2,1,0:T(8,128)(2,1)} %wg_hbm.1, bf16[1,7168,512]{2,1,0:T(8,128)(2,1)} %wu_hbm.1, bf16[1,512,7168]{2,1,0:T(8,128)(2,1)} %wd_hbm.1), custom_call_target="tpu_custom_call" | custom-call | tf_op jit(solution)/shard_map/pallas_call | solution.py:388
  66.6 1.6 %copy.10 = bf16[16,7168]{1,0:T(8,128)(2,1)} copy(bf16[16,7168]{1,0:T(8,128)(2,1)} %get-tuple-element.8) | data formatting | bytes 458752

commit v2 on v1

v2 whole, which is shorter than its diff:
```python
import functools

import jax
import jax.numpy as jnp
from jax import lax
from jax.experimental import pallas as pl
from jax.experimental.pallas import tpu as pltpu
from jax.sharding import PartitionSpec as P

ROUTE_SCALE = 2.5
PRECISE = lax.Precision.HIGHEST


def assignment_slots(flat_routes, experts):
    labels = jnp.arange(experts, dtype=jnp.int32)
    onehot = (flat_routes[:, :, None] == labels[None, None, :]).astype(jnp.int32)
    before = jnp.cumsum(onehot, axis=1) - onehot
    return (jnp.sum(before * onehot, axis=2), jnp.sum(onehot, axis=1))


def pack(members, flat_routes, slot_ids, experts, capacity, top_k):
    blocks, per_block = flat_routes.shape
    tok_dev = per_block // top_k
    member = jnp.arange(blocks, dtype=jnp.int32)[:, None]
    target = ((member * experts + flat_routes) * capacity + slot_ids).reshape(-1)
    source = (member * tok_dev + jnp.arange(per_block, dtype=jnp.int32)[None, :] // top_k).reshape(
        -1
    )
    placing = (
        jnp.arange(blocks * experts * capacity, dtype=jnp.int32)[:, None] == target[None, :]
    ).astype(jnp.bfloat16)
    owners = (source[:, None] == jnp.arange(blocks * tok_dev, dtype=jnp.int32)[None, :]).astype(
        jnp.bfloat16
    )
    picker = jnp.dot(placing, owners, preferred_element_type=jnp.float32).astype(jnp.bfloat16)
    filled = jnp.dot(picker, members, preferred_element_type=jnp.float32).astype(jnp.bfloat16)
    return filled.reshape(blocks, experts, capacity, members.shape[1])


def expert_rows(row_block, gate_w, up_w, down_w):
    gate_act = jnp.dot(row_block, gate_w, preferred_element_type=jnp.float32)
    up_act = jnp.dot(row_block, up_w, preferred_element_type=jnp.float32)
    hidden = (jax.nn.silu(gate_act) * up_act).astype(jnp.bfloat16)
    return jnp.dot(hidden, down_w, preferred_element_type=jnp.float32)


def on_device(tokens, routes, route_logits, gate_weight, up_weight, down_weight):
    tok_dev, top_k = routes.shape
    model_width = tokens.shape[1]
    experts = lax.axis_size("ep")
    groups = lax.axis_size("dp")
    capacity = min(tok_dev // 2, 2 * tok_dev * top_k // experts)
    per_block = tok_dev * top_k
    gate_w = gate_weight[0]
    up_w = up_weight[0]
    down_w = down_weight[0]
    own_flat = routes.reshape(1, per_block)
    own_slots, own_counts = assignment_slots(own_flat, experts)
    buffer = pack(tokens, own_flat, own_slots, experts, capacity, top_k)
    received = lax.all_to_all(buffer, "ep", split_axis=1, concat_axis=1, tiled=True)
    partial_value = expert_rows(
        lax.all_gather(received.reshape(-1, model_width), "dp", axis=0, tiled=True),
        gate_w,
        up_w,
        down_w,
    )
    shares = lax.psum_scatter(
        partial_value.astype(jnp.bfloat16), "dp", scatter_dimension=0, tiled=True
    ).astype(jnp.float32)
    returned = lax.all_to_all(
        shares.reshape(experts, capacity, model_width).astype(jnp.bfloat16),
        "ep",
        split_axis=0,
        concat_axis=0,
        tiled=True,
    ).astype(jnp.float32)
    affinity = jax.nn.sigmoid(route_logits)
    weights = (ROUTE_SCALE * affinity / jnp.sum(affinity, axis=1, keepdims=True)).reshape(-1)
    own_target = own_flat[0] * capacity + own_slots[0]
    spread = jnp.where(
        own_target[:, None] == jnp.arange(experts * capacity, dtype=jnp.int32)[None, :],
        weights[:, None],
        0.0,
    )
    owners = (
        jnp.arange(tok_dev, dtype=jnp.int32)[:, None]
        == jnp.arange(per_block, dtype=jnp.int32)[None, :] // top_k
    ).astype(jnp.float32)
    combine = jnp.dot(owners, spread, precision=PRECISE)
    moe_output = jnp.dot(
        combine, returned.reshape(experts * capacity, model_width), precision=PRECISE
    ).astype(jnp.bfloat16)
    local_counts = own_counts[0].astype(jnp.float32)
    whole = lax.psum(local_counts, ("ep", "dp"))
    expert_count = lax.dynamic_slice_in_dim(whole, lax.axis_index("ep"), 1)
    mean_count = float(tok_dev * groups * top_k)
    expert_load = expert_count / mean_count
    return (moe_output, expert_load)


MESH = pl.DeviceIdType.MESH
RELAY_LAG = 1
X_LAG = 2
MM_LAG = 3
FAR_LAG = 3
FAR_X_LAG = 5
FAR_MM_LAG = 6
HALF_LAG = 1
SUM_EARLY = 3
SUM_LAG = 3
MIX_LAG = 5
OUT_LAG = 7
OUT_NEAR = 5
NEAR_AHEAD = 3
RAW_AHEAD = 1


def chunk_count(width):
    for count in (7, 7, 8, 4, 2):
        if width % (count * 128) == 0:
            return count
    return 1


def remote(src, dst, send, recv, ep, dp):
    return pltpu.make_async_remote_copy(
        src_ref=src,
        dst_ref=dst,
        send_sem=send,
        recv_sem=recv,
        device_id={"ep": ep, "dp": dp},
        device_id_type=MESH,
    )


def landed(ref, sem):
    pltpu.make_async_copy(ref, ref, sem).wait()


def wide(value):
    return value.astype(jnp.float32)


def fused_kernel(
    E, G, cap, nc, dc, mean_count,
    routes_hbm, logits_hbm, tokens_hbm, wg_hbm, wu_hbm, wd_hbm,
    out, load,
    routes, logits, tokens, far_routes, far_logits, far_tokens,
    wgu, wd, picker, combine, slots, rows, acc_g, acc_u, hidden, part,
    a_recv, b_send, b_recv, r_send, r_recv, p_send, p_recv, out_v, load_v,
    cnt_send, cnt_recv, dcnt_send, dcnt_recv,
    in_sem, w_sem, d_sem, t_send, t_recv, m_send, m_recv, s_send, s_recv, x_send, x_recv, c_send, c_recv,
    ra_send, ra_recv, rb_send, rb_recv, rr_send, rr_recv, p_sent, p_got,
    n_send, n_recv, nd_send, nd_recv, o_sem, l_sem,
):
    me = lax.axis_index("ep")
    dp = lax.axis_index("dp")
    hi = dp // 2
    lo = dp % 2
    px = (1 - hi) * 2 + lo
    pc = hi * 2 + (1 - lo)
    diagonal = (1 - hi) * 2 + (1 - lo)
    H = E // 2
    base = (me // H) * H
    mine = me - base
    mirror = lax.rem(me + H, E)
    top, tok = routes_hbm.shape
    n_slots = H * cap
    n_rows = G * n_slots

    def loop(lower, upper, body):
        def step(k, carry):
            body(k)
            return carry

        lax.fori_loop(lower, upper, step, 0)

    others = [jnp.where(mine + k >= H, mine + k - H, mine + k) for k in range(1, H)]

    def peers(body):
        for m in others:
            body(m)

    def ranked(body):
        for k, m in enumerate(others):
            body(k + 1, m)

    def everyone(body):
        loop(1, E, lambda k: body(lax.rem(me + k, E)))

    barrier = pltpu.get_barrier_semaphore()

    def greet(ep, who):
        pl.semaphore_signal(
            barrier, inc=1, device_id={"ep": ep, "dp": who}, device_id_type=MESH)

    greet(mirror, dp)
    peers(lambda m: greet(base + m, dp))
    greet(me, px)
    greet(me, pc)

    def columns(c):
        return pl.ds(pl.multiple_of(c * dc, 128), dc)

    own_routes = pltpu.make_async_copy(routes_hbm, routes, in_sem.at[0])
    own_logits = pltpu.make_async_copy(logits_hbm, logits, in_sem.at[1])
    own_routes.start()
    own_logits.start()
    loop(0, nc, lambda c: pltpu.make_async_copy(
        tokens_hbm.at[:, columns(c)], tokens.at[c], in_sem.at[2]).start())

    def weight_copies(c):
        return (
            pltpu.make_async_copy(wg_hbm.at[0, columns(c)], wgu.at[0, c], w_sem.at[c]),
            pltpu.make_async_copy(wu_hbm.at[0, columns(c)], wgu.at[1, c], w_sem.at[c]),
            pltpu.make_async_copy(wd_hbm.at[0, :, columns(c)], wd.at[c], d_sem),
        )

    def start_weights(c):
        copies = weight_copies(c)
        copies[0].start()
        copies[1].start()

    loop(0, nc, start_weights)
    loop(0, nc, lambda c: weight_copies(c)[2].start())

    def naming(table, first, amount):
        row = lax.broadcasted_iota(jnp.int32, (amount * cap, tok), 0)
        named = jnp.zeros((amount * cap, tok), jnp.float32)
        for k in range(top):
            named = named + jnp.where(table[k:k + 1, :] == first + row // cap, 1.0, 0.0)
        return row, named

    def placing(table):
        row, named = naming(table, base, H)
        earlier = jnp.where(
            lax.broadcasted_iota(jnp.int32, (tok, tok), 0)
            < lax.broadcasted_iota(jnp.int32, (tok, tok), 1), 1.0, 0.0)
        before = jnp.dot(named, earlier, preferred_element_type=jnp.float32)
        return row, named, before == (row % cap).astype(jnp.float32)

    def choose(table, h):
        _, named, placed = placing(table)
        picker[h] = jnp.where(placed, named, 0.0).astype(jnp.bfloat16)

    def weigh(table, scores, h):
        row, _, placed = placing(table)
        affinity = jax.nn.sigmoid(scores[...])
        weights = ROUTE_SCALE * affinity / jnp.sum(affinity, axis=0, keepdims=True)
        spread = jnp.zeros((n_slots, tok), jnp.float32)
        for k in range(top):
            hit = table[k:k + 1, :] == base + row // cap
            spread = spread + jnp.where(hit, weights[k:k + 1, :], 0.0)
        spread = jnp.where(placed, spread, 0.0)
        coarse = spread.astype(jnp.bfloat16)
        rest = spread - wide(coarse)
        middle = rest.astype(jnp.bfloat16)
        fine = (rest - wide(middle)).astype(jnp.bfloat16)
        same = jnp.where(
            lax.broadcasted_iota(jnp.int32, (tok, tok), 0)
            == lax.broadcasted_iota(jnp.int32, (tok, tok), 1), 1.0, 0.0).astype(jnp.bfloat16)
        for i, piece in enumerate((coarse, middle, fine)):
            turned = lax.dot_general(
                same, piece, (((1,), (1,)), ((), ())), preferred_element_type=jnp.float32)
            combine[h, i * tok:(i + 1) * tok] = turned.astype(jnp.bfloat16)

    def pack(source, c, h):
        filled = jnp.dot(picker[h], source[c], preferred_element_type=jnp.float32)
        slots[c, h] = filled.reshape(H, cap, dc).astype(jnp.bfloat16)
        rows[c, h, dp, 0] = slots[c, h, mine]
        across(c, h, slice(0, 1)).start()

    def weighted(c, h):
        got = wide(r_recv[c, h]).reshape(n_slots, dc).astype(jnp.bfloat16)
        mixed = jnp.dot(combine[h], got, preferred_element_type=jnp.float32)
        return mixed[0:tok] + mixed[tok:2 * tok] + mixed[2 * tok:3 * tok]

    def slot_send(c, h, k, m):
        return remote(slots.at[c, h, m], rows.at[c, h, dp, H - k],
                      s_send, s_recv.at[c, h], base + m, dp)

    def raw(c):
        return remote(tokens.at[c], far_tokens.at[c], t_send, t_recv.at[c], mirror, dp)

    def notes():
        return (
            remote(routes, far_routes, m_send.at[0], m_recv.at[0], mirror, dp),
            remote(logits, far_logits, m_send.at[1], m_recv.at[1], mirror, dp),
        )

    def across(c, h, places):
        block = rows.at[c, h, dp, places]
        return remote(block, block, x_send, x_recv.at[c, h], me, px)

    def beside(c, h, who):
        return remote(rows.at[c, h, who], rows.at[c, h, who], c_send, c_recv.at[c, h], me, pc)

    def half(c, h, side):
        return remote(part.at[c, h, side * 2 + (1 - lo)], a_recv.at[c, h, side],
                      ra_send, ra_recv.at[c, h], me, pc)

    def quarter(c, h):
        return remote(b_send.at[c, h], b_recv.at[c, h], rb_send, rb_recv.at[c, h], me, px)

    def back(c, h, k, m):
        return remote(r_send.at[c, h, k], r_recv.at[c, h, mine],
                      rr_send, rr_recv.at[c, h], base + m, dp)

    def share(c):
        return remote(p_send.at[c], p_recv.at[c], p_sent, p_got.at[c], mirror, dp)

    def counts(e):
        return remote(cnt_send.at[e], cnt_recv.at[me], n_send, n_recv, e, dp)

    own_routes.wait()
    choose(routes, 0)
    own_logits.wait()
    landed(tokens, in_sem.at[2])
    pl.semaphore_wait(barrier, H + 2)
    for note in notes():
        note.start()

    def offer(c):
        pack(tokens, c, 0)
        ranked(lambda k, m: slot_send(c, 0, k, m).start())

    near_ahead = min(NEAR_AHEAD, nc)
    raw_ahead = min(RAW_AHEAD, nc)

    def dispatch(c):
        offer(c)
        ratio = near_ahead // raw_ahead

        @pl.when(c % ratio == ratio - 1)
        def _():
            raw(c // ratio).start()

    loop(0, near_ahead, dispatch)
    acc_g[...] = jnp.zeros_like(acc_g)
    acc_u[...] = jnp.zeros_like(acc_u)

    near_start = MM_LAG + nc
    far_start = FAR_MM_LAG + nc
    early = far_start - near_start
    n_items = 2 * nc
    out_start = max(far_start + OUT_LAG, far_start + nc - early + OUT_NEAR)

    def stage(s, lag, amount, body):
        @pl.when((s >= lag) & (s < lag + amount))
        def _():
            body(s - lag)

    def returning(s, lag, early_lag, body):
        a, b = s - early_lag, s - lag
        first = (a >= near_start) & (a < near_start + early)
        later = (b >= far_start) & (b < far_start + n_items - early)

        @pl.when(first | later)
        def _():
            i = jnp.where(first, a - near_start, b - far_start + early)
            far = (i >= early) & (i < early + nc)
            h = jnp.where(far, 1, 0)
            c = jnp.where(i < early, i, jnp.where(far, i - early, i - nc))
            body(h, c)

    def near_in(c):
        landed(rows.at[c, 0, dp, 1:H], s_recv.at[c, 0])
        across(c, 0, slice(1, H)).start()
        beside(c, 0, dp).start()

    def relay(c):
        @pl.when(c == 0)
        def _():
            for note in notes():
                note.wait_recv()
            choose(far_routes, 1)

        landed(far_tokens.at[c], t_recv.at[c])
        pack(far_tokens, c, 1)
        ranked(lambda k, m: slot_send(c, 1, k, m).start())

    def far_in(c):
        landed(rows.at[c, 1, dp, 1:H], s_recv.at[c, 1])
        across(c, 1, slice(1, H)).start()
        beside(c, 1, dp).start()

    def crossed(c, h):
        landed(rows.at[c, h, dp], x_recv.at[c, h])
        beside(c, h, px).start()

    def expand(c, h):

        if h == 0:
            landed(wgu.at[:, c], w_sem.at[c])

        landed(rows.at[c, h, 0:2], c_recv.at[c, h])
        x = wide(rows[c, h]).reshape(n_rows, dc).astype(jnp.bfloat16)
        acc_g[h] += jnp.dot(x, wgu[0, c], preferred_element_type=jnp.float32)
        acc_u[h] += jnp.dot(x, wgu[1, c], preferred_element_type=jnp.float32)

        @pl.when(c == nc - 1)
        def _():
            gate = acc_g[h]
            hidden[h] = (gate / (1.0 + jnp.exp(-gate)) * acc_u[h]).astype(jnp.bfloat16)

    def contract(h, c):
        p = jnp.dot(hidden[h], wd[c], preferred_element_type=jnp.float32)
        part[c, h] = p.reshape(G, H, cap, dc).astype(jnp.bfloat16)
        half(c, h, 1 - hi).start()
        half(c, h, hi).start()

    def pair(h, c):
        landed(a_recv.at[c, h], ra_recv.at[c, h])
        total = wide(part[c, h, px]) + wide(a_recv[c, h, 1 - hi])
        b_send[c, h] = total.astype(jnp.bfloat16)
        quarter(c, h).start()

    def whole(h, c):
        landed(b_recv.at[c, h], rb_recv.at[c, h])
        total = wide(part[c, h, dp]) + wide(a_recv[c, h, hi]) + wide(b_recv[c, h])
        r_send[c, h] = total.astype(jnp.bfloat16)
        ranked(lambda k, m: back(c, h, k, m).start())
        r_recv[c, h, mine] = r_send[c, h, 0]

    def mix(c):
        landed(r_recv.at[c, 1, 0:H - 1], rr_recv.at[c, 1])
        p_send[c] = weighted(c, 1).astype(jnp.bfloat16)
        share(c).start()

    def finish(c):
        landed(r_recv.at[c, 0, 0:H - 1], rr_recv.at[c, 0])
        landed(p_recv.at[c], p_got.at[c])
        out_v[c] = (weighted(c, 0) + wide(p_recv[c])).astype(jnp.bfloat16)
        pltpu.make_async_copy(out_v.at[c], out.at[:, columns(c)], o_sem).start()

    def tally(_):
        _, named = naming(routes, 0, E)
        counted = jnp.sum(named, axis=1, keepdims=True)
        cnt_send[...] = jnp.broadcast_to(counted, (E * cap, 128)).reshape(E, cap, 128)
        cnt_recv[me] = cnt_send[me]
        everyone(lambda e: counts(e).start())

    def gather_counts(_):
        landed(cnt_recv.at[0:E - 1], n_recv)
        total = cnt_recv[0]
        for e in range(1, E):
            total = total + cnt_recv[e]
        dcnt_send[...] = total
        for i in range(1, G):
            remote(dcnt_send, dcnt_recv.at[i - 1], nd_send, nd_recv, me, lax.rem(dp + i, G)).start()

    def loads(_):
        landed(dcnt_recv, nd_recv)
        total = dcnt_send[...]
        for i in range(G - 1):
            total = total + dcnt_recv[i]
        load_v[...] = total[0:1, :] / mean_count
        pltpu.make_async_copy(load_v, load, l_sem).start()

    def weights_of(_):
        weigh(routes, logits, 0)
        weigh(far_routes, far_logits, 1)
        landed(wd, d_sem)

    def main(s):
        stage(s, 0, nc - near_ahead, lambda c: offer(c + near_ahead))
        stage(s, 0, nc - raw_ahead, lambda c: raw(c + raw_ahead).start())
        stage(s, 0, nc, near_in)
        stage(s, RELAY_LAG, nc, relay)
        stage(s, X_LAG, nc, lambda c: crossed(c, 0))
        stage(s, FAR_LAG, nc, far_in)
        stage(s, nc + 2, 1, weights_of)
        stage(s, MM_LAG, nc, lambda c: expand(c, 0))
        stage(s, FAR_X_LAG, nc, lambda c: crossed(c, 1))
        stage(s, FAR_MM_LAG, nc, lambda c: expand(c, 1))
        returning(s, HALF_LAG, HALF_LAG, pair)
        returning(s, 0, 0, contract)
        stage(s, near_start, 1, tally)
        stage(s, far_start + HALF_LAG, 1, gather_counts)
        stage(s, far_start + SUM_LAG + 2, 1, loads)
        returning(s, SUM_LAG, SUM_EARLY, whole)
        stage(s, far_start + MIX_LAG, nc, mix)
        stage(s, out_start, nc, finish)

    loop(0, out_start + nc, main)

    landed(cnt_recv.at[0:E - 1], n_send)
    landed(dcnt_recv, nd_send)
    for note in notes():
        note.wait_send()
    landed(tokens, t_send)
    landed(slots.at[:, :, 0:H - 1], s_send)
    landed(b_send, x_send)
    landed(a_recv, c_send)
    landed(a_recv, ra_send)
    landed(b_send, rb_send)
    landed(r_send.at[:, :, 1:H], rr_send)
    landed(p_send, p_sent)
    pltpu.make_async_copy(load_v, load, l_sem).wait()
    landed(out_v, o_sem)


def fused_device(tokens, routes, route_logits, gate_weight, up_weight, down_weight):
    tok_dev, top_k = routes.shape
    width = tokens.shape[1]
    units = gate_weight.shape[2]
    E = lax.axis_size("ep")
    G = lax.axis_size("dp")
    H = E // 2
    cap = min(tok_dev // 2, 2 * tok_dev * top_k // E)
    nc = chunk_count(width)
    dc = width // nc
    bf, f32 = jnp.bfloat16, jnp.float32
    dma = pltpu.SemaphoreType.DMA
    anywhere = pl.BlockSpec(memory_space=pl.ANY)
    rows = G * H * cap
    moe_output, load = pl.pallas_call(
        functools.partial(fused_kernel, E, G, cap, nc, dc, float(tok_dev * G * top_k)),
        out_shape=(
            jax.ShapeDtypeStruct((tok_dev, width), bf),
            jax.ShapeDtypeStruct((1, 128), f32),
        ),
        in_specs=[anywhere] * 6,
        out_specs=(anywhere, anywhere),
        scratch_shapes=[
            pltpu.VMEM((top_k, tok_dev), jnp.int32),
            pltpu.VMEM((top_k, tok_dev), f32),
            pltpu.VMEM((nc, tok_dev, dc), bf),
            pltpu.VMEM((top_k, tok_dev), jnp.int32),
            pltpu.VMEM((top_k, tok_dev), f32),
            pltpu.VMEM((nc, tok_dev, dc), bf),
            pltpu.VMEM((2, nc, dc, units), bf),
            pltpu.VMEM((nc, units, dc), bf),
            pltpu.VMEM((2, H * cap, tok_dev), bf),
            pltpu.VMEM((2, 3 * tok_dev, H * cap), bf),
            pltpu.VMEM((nc, 2, H, cap, dc), bf),
            pltpu.VMEM((nc, 2, G, H, cap, dc), bf),
            pltpu.VMEM((2, rows, units), f32),
            pltpu.VMEM((2, rows, units), f32),
            pltpu.VMEM((2, rows, units), bf),
            pltpu.VMEM((nc, 2, G, H, cap, dc), bf),
            pltpu.VMEM((nc, 2, 2, H, cap, dc), bf),
            pltpu.VMEM((nc, 2, H, cap, dc), bf),
            pltpu.VMEM((nc, 2, H, cap, dc), bf),
            pltpu.VMEM((nc, 2, H, cap, dc), bf),
            pltpu.VMEM((nc, 2, H, cap, dc), bf),
            pltpu.VMEM((nc, tok_dev, dc), bf),
            pltpu.VMEM((nc, tok_dev, dc), bf),
            pltpu.VMEM((nc, tok_dev, dc), bf),
            pltpu.VMEM((1, 128), f32),
            pltpu.VMEM((E, cap, 128), f32),
            pltpu.VMEM((E, cap, 128), f32),
            pltpu.VMEM((cap, 128), f32),
            pltpu.VMEM((G - 1, cap, 128), f32),
            dma((3,)), dma((nc,)), dma,
            dma, dma((nc,)),
            dma((2,)), dma((2,)),
            dma, dma((nc, 2)),
            dma, dma((nc, 2)),
            dma, dma((nc, 2)),
            dma, dma((nc, 2)),
            dma, dma((nc, 2)),
            dma, dma((nc, 2)),
            dma, dma((nc,)),
            dma, dma,
            dma, dma,
            dma, dma,
        ],
        compiler_params=pltpu.CompilerParams(
            collective_id=0, has_side_effects=True, vmem_limit_bytes=60 * 2**20
        ),
    )(routes.T, route_logits.T, tokens, gate_weight, up_weight, down_weight)
    return moe_output, load[0, :1]


def fits(mesh):
    return mesh.shape["dp"] == 4 and mesh.shape["ep"] in (4, 8)


def solution(mesh):
    body = fused_device if fits(mesh) else on_device
    return jax.shard_map(
        body,
        mesh=mesh,
        in_specs=(
            P(("ep", "dp"), None),
            P(("ep", "dp"), None),
            P(("ep", "dp"), None),
            P("ep", None, "dp"),
            P("ep", None, "dp"),
            P("ep", "dp", None),
        ),
        out_specs=(P(("ep", "dp"), None), P("ep")),
        check_vma=False,
    )
```

time: 70.2 us -> 62.9 us (0.90)
  Pallas kernels: 66 us -> 58.7 us
    pallas_call x1, Pallas kernels: 66 us -> 58.7 us  [fused_device(): pl.pallas_call(functools.partial(fused_kernel, E, G, cap, nc, dc, float(t...]
where the time goes in v2:
time: 62.9 us; the launch traced here: 62.7 us
  Pallas kernels  58.7 us (93%)
  between operations  2.4 us (4%)
  local copies, waits for them, and re-layouts  1.64 us (3%)
    pallas_call x1, Pallas kernels, fused_device(): pl.pallas_call(functools.partial(fused_kernel, E, G, cap, nc, dc, float(t...  58.7 us
    unnamed x1, local copies, waits for them, and re-layouts  1.64 us

profile of v2, /device:TPU:0, one launch (start us, length us, event | category | flops | bytes accessed | tf_op | source)
XLA Modules:
  0.0 62.7 jit_solution(11261028675574091204)
XLA Ops:
  0.6 58.7 %shard_map.77 = (bf16[16,7168]{1,0:T(8,128)(2,1)}, f32[1,128]{1,0:T(1,128)}) custom-call(s32[2,16]{1,0:T(2,128)} %bitcast.4, f32[2,16]{1,0:T(2,128)} %bitcast.5, bf16[16,7168]{1,0:T(8,128)(2,1)} %tokens_hbm.1, bf16[1,7168,512]{2,1,0:T(8,128)(2,1)} %wg_hbm.1, bf16[1,7168,512]{2,1,0:T(8,128)(2,1)} %wu_hbm.1, bf16[1,512,7168]{2,1,0:T(8,128)(2,1)} %wd_hbm.1), custom_call_target="tpu_custom_call" | custom-call | tf_op jit(solution)/shard_map/pallas_call | solution.py:517
  59.3 1.6 %copy.10 = bf16[16,7168]{1,0:T(8,128)(2,1)} copy(bf16[16,7168]{1,0:T(8,128)(2,1)} %get-tuple-element.8) | data formatting | bytes 458752

commit v3 on v2

--- a/solution.py
+++ b/solution.py
@@ -100,12 +100,13 @@
 
 MESH = pl.DeviceIdType.MESH
 RELAY_LAG = 1
+NEAR_LAG = 0
 X_LAG = 2
 MM_LAG = 3
 FAR_LAG = 3
 FAR_X_LAG = 5
 FAR_MM_LAG = 6
-HALF_LAG = 1
+HALF_LAG = 0
 SUM_EARLY = 3
 SUM_LAG = 3
 MIX_LAG = 5
@@ -149,7 +150,7 @@
     wgu, wd, picker, combine, slots, rows, acc_g, acc_u, hidden, part,
     a_recv, b_send, b_recv, r_send, r_recv, p_send, p_recv, out_v, load_v,
     cnt_send, cnt_recv, dcnt_send, dcnt_recv,
-    in_sem, w_sem, d_sem, t_send, t_recv, m_send, m_recv, s_send, s_recv, x_send, x_recv, c_send, c_recv,
+    in_sem, w_sem, d_sem, t_send, t_recv, m_send, m_recv, s_send, s_recv, y_recv, x_send, x_recv, c_send, c_recv,
     ra_send, ra_recv, rb_send, rb_recv, rr_send, rr_recv, p_sent, p_got,
     n_send, n_recv, nd_send, nd_recv, o_sem, l_sem,
 ):
@@ -175,15 +176,13 @@
 
         lax.fori_loop(lower, upper, step, 0)
 
-    others = [jnp.where(mine + k >= H, mine + k - H, mine + k) for k in range(1, H)]
-
-    def peers(body):
-        for m in others:
-            body(m)
-
-    def ranked(body):
-        for k, m in enumerate(others):
-            body(k + 1, m)
+    side, level = mine % 2, mine // 2
+    members = (
+        mine,
+        level * 2 + (1 - side),
+        (1 - level) * 2 + side,
+        (1 - level) * 2 + (1 - side),
+    )
 
     def everyone(body):
         loop(1, E, lambda k: body(lax.rem(me + k, E)))
@@ -195,7 +194,8 @@
             barrier, inc=1, device_id={"ep": ep, "dp": who}, device_id_type=MESH)
 
     greet(mirror, dp)
-    peers(lambda m: greet(base + m, dp))
+    for m in members[1:]:
+        greet(base + m, dp)
     greet(me, px)
     greet(me, pc)
 
@@ -275,9 +275,10 @@
         mixed = jnp.dot(combine[h], got, preferred_element_type=jnp.float32)
         return mixed[0:tok] + mixed[tok:2 * tok] + mixed[2 * tok:3 * tok]
 
-    def slot_send(c, h, k, m):
-        return remote(slots.at[c, h, m], rows.at[c, h, dp, H - k],
-                      s_send, s_recv.at[c, h], base + m, dp)
+    def slot_send(c, h, k):
+        arrived = y_recv.at[c] if (h, k) == (0, 1) else s_recv.at[c, h]
+        return remote(slots.at[c, h, members[k]], rows.at[c, h, dp, k],
+                      s_send, arrived, base + members[k], dp)
 
     def raw(c):
         return remote(tokens.at[c], far_tokens.at[c], t_send, t_recv.at[c], mirror, dp)
@@ -302,9 +303,9 @@
     def quarter(c, h):
         return remote(b_send.at[c, h], b_recv.at[c, h], rb_send, rb_recv.at[c, h], me, px)
 
-    def back(c, h, k, m):
+    def back(c, h, k):
         return remote(r_send.at[c, h, k], r_recv.at[c, h, mine],
-                      rr_send, rr_recv.at[c, h], base + m, dp)
+                      rr_send, rr_recv.at[c, h], base + members[k], dp)
 
     def share(c):
         return remote(p_send.at[c], p_recv.at[c], p_sent, p_got.at[c], mirror, dp)
@@ -320,26 +321,30 @@
     for note in notes():
         note.start()
 
-    def offer(c):
-        pack(tokens, c, 0)
-        ranked(lambda k, m: slot_send(c, 0, k, m).start())
+    def ahead(c):
+        slot_send(c, 0, 2).start()
+        slot_send(c, 0, 3).start()
 
     near_ahead = min(NEAR_AHEAD, nc)
     raw_ahead = min(RAW_AHEAD, nc)
 
     def dispatch(c):
-        offer(c)
-        ratio = near_ahead // raw_ahead
-
-        @pl.when(c % ratio == ratio - 1)
+        pack(tokens, c, 0)
+        slot_send(c, 0, 1).start()
+
+        @pl.when(c < raw_ahead)
         def _():
-            raw(c // ratio).start()
-
-    loop(0, near_ahead, dispatch)
+            raw(c).start()
+
+        @pl.when(c < near_ahead)
+        def _():
+            ahead(c)
+
+    loop(0, nc, dispatch)
     acc_g[...] = jnp.zeros_like(acc_g)
     acc_u[...] = jnp.zeros_like(acc_u)
 
-    near_start = MM_LAG + nc
+    near_start = MM_LAG + nc - 1
     far_start = FAR_MM_LAG + nc
     early = far_start - near_start
     n_items = 2 * nc
@@ -363,9 +368,13 @@
             c = jnp.where(i < early, i, jnp.where(far, i - early, i - nc))
             body(h, c)
 
+    def beside_in(c):
+        landed(rows.at[c, 0, dp, 1], y_recv.at[c])
+        across(c, 0, slice(1, 2)).start()
+
     def near_in(c):
-        landed(rows.at[c, 0, dp, 1:H], s_recv.at[c, 0])
-        across(c, 0, slice(1, H)).start()
+        landed(rows.at[c, 0, dp, 2:H], s_recv.at[c, 0])
+        across(c, 0, slice(2, H)).start()
         beside(c, 0, dp).start()
 
     def relay(c):
@@ -377,7 +386,8 @@
 
         landed(far_tokens.at[c], t_recv.at[c])
         pack(far_tokens, c, 1)
-        ranked(lambda k, m: slot_send(c, 1, k, m).start())
+        for k in range(1, H):
+            slot_send(c, 1, k).start()
 
     def far_in(c):
         landed(rows.at[c, 1, dp, 1:H], s_recv.at[c, 1])
@@ -419,7 +429,8 @@
         landed(b_recv.at[c, h], rb_recv.at[c, h])
         total = wide(part[c, h, dp]) + wide(a_recv[c, h, hi]) + wide(b_recv[c, h])
         r_send[c, h] = total.astype(jnp.bfloat16)
-        ranked(lambda k, m: back(c, h, k, m).start())
+        for k in range(1, H):
+            back(c, h, k).start()
         r_recv[c, h, mine] = r_send[c, h, 0]
 
     def mix(c):
@@ -463,24 +474,25 @@
         landed(wd, d_sem)
 
     def main(s):
-        stage(s, 0, nc - near_ahead, lambda c: offer(c + near_ahead))
         stage(s, 0, nc - raw_ahead, lambda c: raw(c + raw_ahead).start())
-        stage(s, 0, nc, near_in)
+        stage(s, 0, nc - near_ahead, lambda c: ahead(c + near_ahead))
+        stage(s, 0, nc, beside_in)
+        stage(s, NEAR_LAG, nc, near_in)
         stage(s, RELAY_LAG, nc, relay)
         stage(s, X_LAG, nc, lambda c: crossed(c, 0))
         stage(s, FAR_LAG, nc, far_in)
         stage(s, nc + 2, 1, weights_of)
         stage(s, MM_LAG, nc, lambda c: expand(c, 0))
+        returning(s, 0, 0, contract)
+        stage(s, near_start, 1, tally)
         stage(s, FAR_X_LAG, nc, lambda c: crossed(c, 1))
         stage(s, FAR_MM_LAG, nc, lambda c: expand(c, 1))
+        returning(s, SUM_LAG, SUM_EARLY, whole)
+        stage(s, far_start + 1, 1, gather_counts)
+        stage(s, far_start + MIX_LAG, nc, mix)
+        stage(s, far_start + SUM_LAG + 2, 1, loads)
+        stage(s, out_start, nc, finish)
         returning(s, HALF_LAG, HALF_LAG, pair)
-        returning(s, 0, 0, contract)
-        stage(s, near_start, 1, tally)
-        stage(s, far_start + HALF_LAG, 1, gather_counts)
-        stage(s, far_start + SUM_LAG + 2, 1, loads)
-        returning(s, SUM_LAG, SUM_EARLY, whole)
-        stage(s, far_start + MIX_LAG, nc, mix)
-        stage(s, out_start, nc, finish)
 
     loop(0, out_start + nc, main)
 
@@ -555,7 +567,7 @@
             dma((3,)), dma((nc,)), dma,
             dma, dma((nc,)),
             dma((2,)), dma((2,)),
-            dma, dma((nc, 2)),
+            dma, dma((nc, 2)), dma((nc,)),
             dma, dma((nc, 2)),
             dma, dma((nc, 2)),
             dma, dma((nc, 2)),
@@ -574,7 +586,7 @@
 
 
 def fits(mesh):
-    return mesh.shape["dp"] == 4 and mesh.shape["ep"] in (4, 8)
+    return mesh.shape["dp"] == 4 and mesh.shape["ep"] == 8
 
 
 def solution(mesh):

time: 62.9 us -> 61.3 us (0.975)
  Pallas kernels: 58.7 us -> 57 us
    pallas_call x1, Pallas kernels: 58.7 us -> 57 us  [fused_device(): pl.pallas_call(functools.partial(fused_kernel, E, G, cap, nc, dc, float(t...]
where the time goes in v3:
time: 61.3 us; the launch traced here: 61.1 us
  Pallas kernels  57 us (93%)
  between operations  2.4 us (4%)
  local copies, waits for them, and re-layouts  1.64 us (3%)
    pallas_call x1, Pallas kernels, fused_device(): pl.pallas_call(functools.partial(fused_kernel, E, G, cap, nc, dc, float(t...  57 us
    unnamed x1, local copies, waits for them, and re-layouts  1.64 us

profile of v3, /device:TPU:0, one launch (start us, length us, event | category | flops | bytes accessed | tf_op | source)
XLA Modules:
  0.0 61.1 jit_solution(14023080230276450348)
XLA Ops:
  0.6 57.0 %shard_map.77 = (bf16[16,7168]{1,0:T(8,128)(2,1)}, f32[1,128]{1,0:T(1,128)}) custom-call(s32[2,16]{1,0:T(2,128)} %bitcast.4, f32[2,16]{1,0:T(2,128)} %bitcast.5, bf16[16,7168]{1,0:T(8,128)(2,1)} %tokens_hbm.1, bf16[1,7168,512]{2,1,0:T(8,128)(2,1)} %wg_hbm.1, bf16[1,7168,512]{2,1,0:T(8,128)(2,1)} %wu_hbm.1, bf16[1,512,7168]{2,1,0:T(8,128)(2,1)} %wd_hbm.1), custom_call_target="tpu_custom_call" | custom-call | tf_op jit(solution)/shard_map/pallas_call | solution.py:529
  57.7 1.6 %copy.10 = bf16[16,7168]{1,0:T(8,128)(2,1)} copy(bf16[16,7168]{1,0:T(8,128)(2,1)} %get-tuple-element.8) | data formatting | bytes 458752
